TPU v7x, 32 devices: a whole 2x2x4 slice. The times are simulated.
32 devices in a mesh: gx: 4 (over x, core), gy: 4 (over z), gz: 2 (over y).
Axes of the slice: x: 2, y: 2, z: 4, core: 2. Of those that a mesh axis runs over, the one named last changes fastest.
Arguments:
- fields: float32 [11, 500, 32, 256], P(None, 'gx', 'gy', 'gz'), may hold values from -6 to 6
- var_scale: float32 [11], replicated, may hold values from 0.3 to 3
- start_basis: float32 [500, 64], replicated, may hold values from -6 to 6
Outputs:
- factor: float32 [500, 64], replicated
- core: float32 [64, 11, 32, 256], P('gx', None, 'gy', 'gz')
All inputs are finite; a program needn't handle non-finite values.
Results may differ from a plain program's by a relative error of at most 0.0002.
Values sent between devices are 32-bit elements; how exact they have to be, the bound alone decides.
A program may use at most 128 MiB of HBM per device.

v0:
```python
import jax
import jax.numpy as jnp
from jax import lax
from jax.sharding import PartitionSpec as P

ITERS = 3


def orthonormal(block):
    small = jnp.dot(block.T, block, precision=lax.Precision.HIGHEST)
    lower = jnp.linalg.cholesky(small)
    return jax.scipy.linalg.solve_triangular(lower, block.T, lower=True).T


def per_device(fields, var_scale, start_basis):
    scaled = fields * var_scale[:, None, None, None]
    rows_dev = scaled.shape[1]
    contract = (((0, 2, 3), (0, 2, 3)), ((), ()))
    swapped = lax.all_to_all(scaled, "gx", split_axis=2, concat_axis=1, tiled=True)
    partial_gram = lax.dot_general(swapped, swapped, contract, precision=lax.Precision.HIGHEST)
    gram = lax.psum(partial_gram, ("gx", "gy", "gz"))
    basis = start_basis
    for step in range(ITERS):
        basis = orthonormal(jnp.dot(gram, basis, precision=lax.Precision.HIGHEST))
    along_rows = (((0,), (1,)), ((), ()))
    own_basis = lax.dynamic_slice_in_dim(basis, lax.axis_index("gx") * rows_dev, rows_dev, 0)
    core = lax.psum_scatter(
        lax.dot_general(own_basis, scaled, along_rows, precision=lax.Precision.HIGHEST),
        "gx",
        scatter_dimension=0,
        tiled=True,
    )
    return (basis, core)


def solution(mesh):
    in_specs = (P(None, "gx", "gy", "gz"), P(), P())
    out_specs = (P(), P("gx", None, "gy", "gz"))
    return jax.shard_map(
        per_device, mesh=mesh, in_specs=in_specs, out_specs=out_specs, check_vma=False
    )
```

profile of v0, /device:TPU:0, one launch (start us, length us, event | category | flops | bytes accessed | tf_op | source)
XLA Modules:
  0.0 333.2 jit_solution(15597270235788873526)
XLA Ops:
  7.2 0.0 copy-start
  7.2 0.0 all-reduce.2.cloned.1.call-start
  7.2 3.1 broadcast_multiply_fusion
  10.3 0.0 copy-start.1
  10.3 1.1 copy.24
  11.4 1.3 copy-done.1
  12.7 69.0 %all_to_all.18 = f32[11,125,8,128]{3,1,0,2:T(8,128)S(1)} all-to-all(f32[11,125,8,128]{3,1,0,2:T(8,128)S(1)} %copy.24), channel_id=1, replica_groups=mesh['gx'=4,'gy'=4,'gz'=2] {'gx'}, dimensions={2} | all-to-all | bytes 11264000 | tf_op jit(solution)/shard_map/all_to_all | solution.py:19
  81.7 2.9 copy.36
  84.6 6.2 %all_to_all.16 = f32[11,500,2,128]{3,1,2,0:T(8,128)} reshape(f32[11,4,125,2,128]{4,2,1,3,0:T(8,128)} %bitcast.67) | data formatting | bytes 11264000 | tf_op jit(solution)/shard_map/all_to_all | solution.py:19
  90.8 13.6 %convolution_bitcast_fusion = f32[500,500]{1,0:T(8,128)} fusion(f32[11,500,2,128]{3,1,2,0:T(8,128)} %all_to_all.16), kind=kOutput, calls=%fused_computation.4 | convolution fusion | flops 8448000000 | bytes 6632000 | tf_op jit(solution)/shard_map/dot_general | solution.py:20
  104.4 0.0 all-reduce.2.cloned.1.call-update
  104.4 0.2 reduce-scatter.2.cloned.1.call-start
  104.7 130.7 %all-reduce.2.cloned.1.call-done = f32[500,500]{1,0:T(8,128)} async-done(((f32[500,500]{1,0:T(8,128)}), f32[500,500]{1,0:T(8,128)}) %all-reduce.2.cloned.1.call-update) | async-done | bytes 1000016 | tf_op jit(solution)/shard_map/psum | solution.py:21
  235.4 0.0 copy-done
  235.4 2.3 fusion.24
  237.7 0.3 fusion.25
  238.0 0.1 copy.26
  238.0 5.8 %cholesky.59 = f32[64,64]{1,0:T(8,128)S(1)} custom-call(f32[64,64]{1,0:T(8,128)S(1)} %fusion.17), custom_call_target="Cholesky" | custom-call | tf_op jit(solution)/shard_map/jit(cholesky)/cholesky | solution.py:11
  243.9 0.6 compare_reduce_fusion.2
  244.6 0.7 fusion.8
  245.2 4.9 %custom-call.7 = f32[1,64,64]{1,2,0:T(8,128)S(1)} custom-call(f32[1,64,64]{2,1,0:T(8,128)S(1)} %fusion.8), custom_call_target="InvertDiagBlocksLowerTriangular" | custom-call | tf_op jit(solution)/shard_map/jit(_solve_triangular)/triangular_solve | solution.py:12
  250.1 0.3 fusion.6
  250.5 2.3 fusion.26
  252.8 0.3 fusion.27
  253.0 0.1 copy.27
  253.1 5.8 %cholesky.70 = f32[64,64]{1,0:T(8,128)S(1)} custom-call(f32[64,64]{1,0:T(8,128)S(1)} %fusion.15), custom_call_target="Cholesky" | custom-call | tf_op jit(solution)/shard_map/jit(cholesky)/cholesky | solution.py:11
  259.0 0.6 compare_reduce_fusion.1
  259.6 0.7 fusion.9
  260.3 4.9 %custom-call.8 = f32[1,64,64]{1,2,0:T(8,128)S(1)} custom-call(f32[1,64,64]{2,1,0:T(8,128)S(1)} %fusion.9), custom_call_target="InvertDiagBlocksLowerTriangular" | custom-call | tf_op jit(solution)/shard_map/jit(_solve_triangular)/triangular_solve | solution.py:12
  265.2 0.3 fusion.4
  265.5 2.3 fusion.28
  267.8 0.3 fusion.29
  268.1 0.1 copy.28
  268.2 5.8 %cholesky.81 = f32[64,64]{1,0:T(8,128)S(1)} custom-call(f32[64,64]{1,0:T(8,128)S(1)} %fusion.13), custom_call_target="Cholesky" | custom-call | tf_op jit(solution)/shard_map/jit(cholesky)/cholesky | solution.py:11
  274.1 0.6 compare_reduce_fusion
  274.7 0.7 fusion.10
  275.4 4.9 %custom-call.9 = f32[1,64,64]{1,2,0:T(8,128)S(1)} custom-call(f32[1,64,64]{2,1,0:T(8,128)S(1)} %fusion.10), custom_call_target="InvertDiagBlocksLowerTriangular" | custom-call | tf_op jit(solution)/shard_map/jit(_solve_triangular)/triangular_solve | solution.py:12
  280.3 0.3 fusion.2
  280.6 0.0 copy-start.2
  280.6 8.3 %fusion = f32[64,11,8,128]{3,0,2,1:T(8,128)} fusion(f32[11,125,8,128]{3,2,1,0:T(8,128)} %copy-done.1, f32[64,500]{1,0:T(8,128)S(1)} %fusion.2, s32[]{:T(128)S(6)} %select_n.6), kind=kOutput, calls=%fused_computation | convolution fusion | flops 1081344000 | bytes 8548356 | tf_op jit(solution)/shard_map/dot_general | solution.py:28
  288.9 0.0 reduce-scatter.2.cloned.1.call-update
  288.9 0.0 copy-done.2
  288.9 35.2 %reduce-scatter.2.cloned.1.call-done = f32[16,11,8,128]{3,0,2,1:T(8,128)} async-done(((f32[64,11,8,128]{3,0,2,1:T(8,128)}), f32[16,11,8,128]{3,0,2,1:T(8,128)}) %reduce-scatter.2.cloned.1.call-update) | async-done | bytes 720912 | tf_op jit(solution)/shard_map/reduce_scatter | solution.py:27
  324.2 2.2 copy.30
  (6 shorter events, 0.1 us)
Async XLA Ops:
  7.2 228.2 %copy-start = (f32[500,64]{0,1:T(8,128)S(1)}, f32[500,64]{0,1:T(8,128)}, u32[]{:S(2)}) copy-start(f32[500,64]{0,1:T(8,128)} %param.8) | copy-start | bytes 384004
  7.2 228.2 %all-reduce.2.cloned.1.call-start = ((), (), s32[]{:S(2)}) async-start(), calls=%async_computation.2 | async-start | bytes 2064384 | tf_op jit(solution)/shard_map/psum | solution.py:21
  10.3 2.4 copy-start.1
  104.4 219.7 %reduce-scatter.2.cloned.1.call-start = ((), (), s32[]{:S(2)}) async-start(), calls=%async_computation.3 | async-start | bytes 3604480 | tf_op jit(solution)/shard_map/reduce_scatter | solution.py:27
  280.6 8.3 %copy-start.2 = (f32[64,500]{1,0:T(8,128)}, f32[64,500]{1,0:T(8,128)S(1)}, u32[]{:S(2)}) copy-start(f32[64,500]{1,0:T(8,128)S(1)} %fusion.2) | copy-start | bytes 384004
Sparse Core Ops, SparseCore 0:
  104.6 130.7 all-reduce.1
  289.0 35.0 reduce-scatter.1
where the time goes:
time: 334 us; the launch traced here: 333 us
  waiting for transfers between devices  166 us (50%)
  blocking collectives  69 us (21%)
  other arithmetic  39.3 us (12%)
  matrix products  30.5 us (9%)
  between operations  14.2 us (4%)
  local copies, waits for them, and re-layouts  13.9 us (4%)
    psum x1, waiting for transfers between devices, per_device(): gram = lax.psum(partial_gram, ('gx', 'gy', 'gz'))  131 us
    all_to_all x1, blocking collectives, per_device(): lax.all_to_all(scaled, 'gx', split_axis=2, concat_axis=1, tiled=True)  69 us
    reduce_scatter x1, waiting for transfers between devices, per_device(): lax.psum_scatter(lax.dot_general(own_basis, scaled, along_rows, precision...  35.2 us
    another operation x9, other arithmetic, orthonormal(): lower = jnp.linalg.cholesky(small)  19.6 us
    another operation x6, other arithmetic, orthonormal(): return jax.scipy.linalg.solve_triangular(lower, block.T, lower=True).T  16.6 us
    dot_general x1, matrix products, per_device(): lax.dot_general(swapped, swapped, contract, precision=lax.Precision.HIGHEST)  13.6 us
    all_to_all x2, local copies, waits for them, and re-layouts, per_device(): lax.all_to_all(scaled, 'gx', split_axis=2, concat_axis=1, tiled=True)  9.05 us
    dot_general x1, matrix products, per_device(): lax.dot_general(own_basis, scaled, along_rows, precision=lax.Precision.HI...  8.26 us
  transfers between devices with their start and end apart: 2, of which 2 were waited for; matrix products, arithmetic and copies ran while one was open for 0% of the time, Pallas kernels for 0%

commit v1 on v0

v1 whole, which is shorter than its diff:
```python
import functools

import jax
import jax.numpy as jnp
from jax import lax
from jax.experimental import pallas as pl
from jax.experimental.pallas import tpu as pltpu
from jax.sharding import PartitionSpec as P

ITERS = 3
LANES = 128
SUB = 8
PANEL = 8
HIGHEST = lax.Precision.HIGHEST
MESH = pl.DeviceIdType.MESH


def flat_index(axes, sizes):
    flat = 0
    for name, size in zip(axes, sizes):
        flat = flat * size + lax.axis_index(name)
    return flat


def coords(flat, sizes):
    out = []
    for size in reversed(sizes):
        out.append(lax.rem(flat, size))
        flat = lax.div(flat, size)
    return tuple(reversed(out))


def reduce_kernel(axes, sizes, owners, rows, g_ref, out_ref, recv, own, s1, r1, s2, r2):
    n = 1
    for size in sizes:
        n *= size
    me = flat_index(axes, sizes)
    barrier = pltpu.get_barrier_semaphore()

    def greet(k, c):
        peer = lax.rem(me + k, n)
        pl.semaphore_signal(barrier, inc=1, device_id=coords(peer, sizes), device_id_type=MESH)
        return c

    lax.fori_loop(1, n, greet, 0)
    pl.semaphore_wait(barrier, n - 1)

    def part(peer):
        return pltpu.make_async_remote_copy(
            src_ref=g_ref.at[peer],
            dst_ref=recv.at[me],
            send_sem=s1.at[peer],
            recv_sem=r1.at[me],
            device_id=coords(peer, sizes),
            device_id_type=MESH,
        )

    def part_from(peer):
        return pltpu.make_async_remote_copy(
            src_ref=g_ref.at[0],
            dst_ref=recv.at[peer],
            send_sem=s1.at[peer],
            recv_sem=r1.at[peer],
            device_id=coords(peer, sizes),
            device_id_type=MESH,
        )

    def whole(peer):
        return pltpu.make_async_remote_copy(
            src_ref=own,
            dst_ref=out_ref.at[me],
            send_sem=s2.at[peer],
            recv_sem=r2.at[me],
            device_id=coords(peer, sizes),
            device_id_type=MESH,
        )

    def whole_from(peer):
        return pltpu.make_async_remote_copy(
            src_ref=own,
            dst_ref=out_ref.at[peer],
            send_sem=s2.at[peer],
            recv_sem=r2.at[peer],
            device_id=coords(peer, sizes),
            device_id_type=MESH,
        )

    def each(do, only_owners):
        def step(k, c):
            peer = lax.rem(me + k, n)
            if only_owners and owners < n:
                pl.when(peer < owners)(lambda: do(peer))
            else:
                do(peer)
            return c

        lax.fori_loop(1, n, step, 0)

    def if_owner(do):
        if owners < n:
            pl.when(me < owners)(do)
        else:
            do()

    each(lambda peer: part(peer).start(), True)

    @if_owner
    def _():
        each(lambda peer: part_from(peer).wait_recv(), False)
        recv[pl.ds(me, 1)] = g_ref[pl.ds(me, 1)]
        own[...] = jnp.sum(recv[...], axis=0)
        each(lambda peer: whole(peer).start(), False)
        out_ref[pl.ds(me, 1)] = own[...][None]

    each(lambda peer: part(peer).wait_send(), True)
    each(lambda peer: whole_from(peer).wait_recv(), True)

    @if_owner
    def _():
        each(lambda peer: whole(peer).wait_send(), False)


def all_reduce_rows(packed, axes, sizes):
    n = 1
    for size in sizes:
        n *= size
    total = packed.shape[0]
    rows = -(-total // (n * SUB)) * SUB
    owners = -(-total // rows)
    packed = jnp.pad(packed, ((0, owners * rows - total), (0, 0))).reshape(owners, rows, LANES)
    out = pl.pallas_call(
        functools.partial(reduce_kernel, axes, sizes, owners, rows),
        out_shape=jax.ShapeDtypeStruct((owners, rows, LANES), jnp.float32),
        in_specs=[pl.BlockSpec(memory_space=pltpu.VMEM)],
        out_specs=pl.BlockSpec(memory_space=pltpu.VMEM),
        scratch_shapes=[
            pltpu.VMEM((n, rows, LANES), jnp.float32),
            pltpu.VMEM((rows, LANES), jnp.float32),
            pltpu.SemaphoreType.DMA((n,)),
            pltpu.SemaphoreType.DMA((n,)),
            pltpu.SemaphoreType.DMA((n,)),
            pltpu.SemaphoreType.DMA((n,)),
        ],
        compiler_params=pltpu.CompilerParams(collective_id=0, has_side_effects=True),
    )(packed)
    return out.reshape(owners * rows, LANES)[:total]


def full(x):
    return jnp.broadcast_to(x, (SUB, LANES))


def inverse_lower(m, rank):
    groups = rank // SUB
    left = LANES - rank
    tiles = [m[g * SUB:(g + 1) * SUB, :] for g in range(groups)]
    sub = lax.broadcasted_iota(jnp.int32, (SUB, LANES), 0)
    done = []
    for g0 in range(groups):
        base = g0 * SUB
        cols = [
            [full(tiles[g][:, left + base + k:left + base + k + 1]) for g in range(g0, groups)]
            for k in range(SUB)
        ]
        rows = [full(tiles[g0][k:k + 1, :]) for k in range(SUB)]
        out = jnp.zeros((SUB, LANES), jnp.float32)
        for a in range(SUB):
            pivot = full(cols[a][0][a:a + 1, :])
            inv = 1.0 / pivot
            row = rows[a] * inv
            out = jnp.where(sub == a, rows[a] * lax.rsqrt(pivot), out)
            for b in range(a + 1, SUB):
                f = full(cols[a][0][b:b + 1, :])
                rows[b] = rows[b] - f * row
                fi = f * inv
                cols[b] = [cb - ca * fi for cb, ca in zip(cols[b], cols[a])]
            for i, g in enumerate(range(g0 + 1, groups)):
                tiles[g] = tiles[g] - cols[a][i + 1] * row
        done.append(out)
    return jnp.concatenate(done, axis=0)[:, :rank]


def iterate_kernel(m, rank, cells, p_ref, start_ref, bt_ref, f_ref, gram, wide):
    t = 0
    for i in range(m):
        for j in range(i, m):
            block = p_ref[t * LANES:(t + 1) * LANES, :]
            gram[i * LANES:(i + 1) * LANES, j * LANES:(j + 1) * LANES] = block
            if i != j:
                gram[j * LANES:(j + 1) * LANES, i * LANES:(i + 1) * LANES] = block.T
            t += 1
    wide[...] = jnp.zeros_like(wide)
    bt_ref[...] = start_ref[...]
    eye = (
        lax.broadcasted_iota(jnp.int32, (rank, LANES), 0)
        == lax.broadcasted_iota(jnp.int32, (rank, LANES), 1)
    ).astype(jnp.float32)

    def step(_, c):
        block = jnp.dot(bt_ref[...], gram[...], precision=HIGHEST, preferred_element_type=jnp.float32)
        wide[LANES - rank:, :] = block
        small = lax.dot_general(
            block, wide[...], (((1,), (1,)), ((), ())), precision=HIGHEST, preferred_element_type=jnp.float32
        )
        lower_inv = inverse_lower(small + eye, rank)
        bt_ref[...] = jnp.dot(lower_inv, block, precision=HIGHEST, preferred_element_type=jnp.float32)
        return c

    lax.fori_loop(0, ITERS, step, 0)
    f_ref[...] = bt_ref[...].T[:cells, :]


def iterate(packed, start_basis, m):
    cells, rank = start_basis.shape
    size = m * LANES
    start = jnp.pad(start_basis.T, ((0, 0), (0, size - cells)))
    vmem = pl.BlockSpec(memory_space=pltpu.VMEM)
    return pl.pallas_call(
        functools.partial(iterate_kernel, m, rank, cells),
        out_shape=(
            jax.ShapeDtypeStruct((rank, size), jnp.float32),
            jax.ShapeDtypeStruct((cells, rank), jnp.float32),
        ),
        in_specs=[vmem, vmem],
        out_specs=(vmem, vmem),
        scratch_shapes=[
            pltpu.VMEM((size, size), jnp.float32),
            pltpu.VMEM((LANES, size), jnp.float32),
        ],
    )(packed, start)


def solution(mesh):
    axes = tuple(mesh.axis_names)
    sizes = tuple(mesh.shape[a] for a in axes)

    def per_device(fields, var_scale, start_basis):
        scaled = fields * var_scale[:, None, None, None]
        contract = (((0, 2, 3), (0, 2, 3)), ((), ()))
        swapped = lax.all_to_all(scaled, "gx", split_axis=2, concat_axis=1, tiled=True)
        partial_gram = lax.dot_general(swapped, swapped, contract, precision=HIGHEST)
        cells = partial_gram.shape[0]
        m = -(-cells // LANES)
        pad = m * LANES - cells
        padded = jnp.pad(partial_gram, ((0, pad), (0, pad)))
        packed = jnp.concatenate(
            [
                padded[i * LANES:(i + 1) * LANES, j * LANES:(j + 1) * LANES]
                for i in range(m)
                for j in range(i, m)
            ],
            axis=0,
        )
        packed = all_reduce_rows(packed, axes, sizes)
        basis_t, factor = iterate(packed, start_basis, m)
        share = lax.dot_general(
            basis_t[:, :cells], swapped, (((1,), (1,)), ((), ())), precision=lax.Precision.HIGH
        )
        core = lax.all_to_all(share, "gx", split_axis=0, concat_axis=2, tiled=True)
        return factor, core

    in_specs = (P(None, "gx", "gy", "gz"), P(), P())
    out_specs = (P(), P("gx", None, "gy", "gz"))
    return jax.shard_map(
        per_device, mesh=mesh, in_specs=in_specs, out_specs=out_specs, check_vma=False
    )
```

time: 334 us -> 177 us (0.53)
  waiting for transfers between devices: 166 us -> 75.3 us
  blocking collectives: 69 us -> 0 us
  Pallas kernels: 0 us -> 50.7 us
  other arithmetic: 39.3 us -> 3.03 us
  between operations: 14.2 us -> 0.77 us
  matrix products: 30.5 us -> 17.9 us
  starting transfers between devices: 0.26 us -> 8.76 us
  local copies, waits for them, and re-layouts: 13.9 us -> 20.6 us
    psum x1 -> x0, waiting for transfers between devices: 131 us -> none  [per_device(): gram = lax.psum(partial_gram, ('gx', 'gy', 'gz'))]
    all_to_all x0 -> x2, waiting for transfers between devices: none -> 75.3 us  [the longest x1 65.1 us: per_device(): lax.all_to_all(scaled, 'gx', split_axis=2, concat_axis=1, tiled=True)]
    all_to_all x1 -> x0, blocking collectives: 69 us -> none  [per_device(): lax.all_to_all(scaled, 'gx', split_axis=2, concat_axis=1, tiled=True)]
    pallas_call x0 -> x2, Pallas kernels: none -> 50.7 us  [the longest x1 39.2 us: all_reduce_rows(): pl.pallas_call(functools.partial(reduce_kernel, axes, sizes, owners, rows...]
    another operation x15 -> x0, other arithmetic: 36.2 us -> none  [the longest x9 19.6 us: orthonormal(): lower = jnp.linalg.cholesky(small)]
    reduce_scatter x1 -> x0, waiting for transfers between devices: 35.2 us -> none  [per_device(): lax.psum_scatter(lax.dot_general(own_basis, scaled, along_rows, precision...]
    dot_general x8 -> x2, matrix products: 29.5 us -> 17.9 us  [the longest x1 13.2 us: per_device(): lax.dot_general(swapped, swapped, contract, precision=HIGHEST)]
    all_to_all x0 -> x2, starting transfers between devices: none -> 8.76 us  [the longest x1 5.27 us: per_device(): lax.all_to_all(scaled, 'gx', split_axis=2, concat_axis=1, tiled=True)]
  transfers between devices with their start and end apart: 2 -> 2, of which waited for: 2 -> 2; matrix products, arithmetic and copies ran while one was open for 0% -> 1% of each run, Pallas kernels for 0% -> 0%
where the time goes in v1:
time: 177 us
  waiting for transfers between devices  75.3 us (43%)
  Pallas kernels  50.7 us (29%)
  local copies, waits for them, and re-layouts  20.6 us (12%)
  matrix products  17.9 us (10%)
  starting transfers between devices  8.76 us (5%)
  other arithmetic  3.03 us (2%)
    all_to_all x1, waiting for transfers between devices, per_device(): lax.all_to_all(scaled, 'gx', split_axis=2, concat_axis=1, tiled=True)  65.1 us
    pallas_call x1, Pallas kernels, all_reduce_rows(): pl.pallas_call(functools.partial(reduce_kernel, axes, sizes, owners, rows...  39.2 us
    dot_general x1, matrix products, per_device(): lax.dot_general(swapped, swapped, contract, precision=HIGHEST)  13.2 us
    all_to_all x2, local copies, waits for them, and re-layouts, per_device(): lax.all_to_all(scaled, 'gx', split_axis=2, concat_axis=1, tiled=True)  12.1 us
    pallas_call x1, Pallas kernels, iterate(): pl.pallas_call(functools.partial(iterate_kernel, m, rank, cells), out_sha...  11.5 us
    all_to_all x1, waiting for transfers between devices, per_device(): core = lax.all_to_all(share, 'gx', split_axis=0, concat_axis=2, tiled=True)  10.2 us
    all_to_all x1, starting transfers between devices, per_device(): lax.all_to_all(scaled, 'gx', split_axis=2, concat_axis=1, tiled=True)  5.27 us
    dot_general x1, matrix products, per_device(): lax.dot_general(basis_t[:, :cells], swapped, (((1,), (1,)), ((), ())), pr...  4.64 us
  transfers between devices with their start and end apart: 2, of which 2 were waited for; matrix products, arithmetic and copies ran while one was open for 1% of the time, Pallas kernels for 0%

profile of v1, /device:TPU:0, one launch (start us, length us, event | category | flops | bytes accessed | tf_op | source)
XLA Modules:
  0.0 177.0 jit_solution(17443843190508235600)
XLA Ops:
  0.6 3.0 %broadcast_multiply_fusion = f32[11,125,8,128]{3,2,1,0:T(8,128)S(1)} fusion(f32[11,125,8,128]{3,2,1,0:T(8,128)} %param.3, f32[11]{0:T(128)} %param.4), kind=kLoop, calls=%fused_computation.1 | loop fusion | flops 1408000 | bytes 11264044 | tf_op jit(solution)/shard_map/mul | solution.py:238
  3.7 3.6 %copy.16 = f32[11,125,8,128]{3,1,0,2:T(8,128)} copy(f32[11,125,8,128]{3,2,1,0:T(8,128)S(1)} %broadcast_multiply_fusion) | data formatting | bytes 11264000 | tf_op jit(solution)/shard_map/mul | solution.py:238
  7.3 0.0 copy-start.2
  7.3 5.3 %all-to-all-start = ((f32[11,125,8,128]{3,1,0,2:T(8,128)}), f32[11,125,8,128]{3,1,0,2:T(8,128)}, u32[]{:S(2)}, u32[]{:S(2)}) async-start(f32[11,125,8,128]{3,1,0,2:T(8,128)} %copy.16), calls=%async_computation | async-start | bytes 11534336 | tf_op jit(solution)/shard_map/all_to_all | solution.py:240
  12.5 0.0 copy-done.2
  12.5 0.7 pad.9.start_ref
  13.2 65.1 %all-to-all-done = f32[11,125,8,128]{3,1,0,2:T(8,128)} async-done(((f32[11,125,8,128]{3,1,0,2:T(8,128)}), f32[11,125,8,128]{3,1,0,2:T(8,128)}, u32[]{:S(2)}, u32[]{:S(2)}) %all-to-all-start) | async-done | bytes 5632032 | tf_op jit(solution)/shard_map/all_to_all | solution.py:240
  78.3 5.9 %copy.24 = f32[11,125,4,2,128]{4,1,2,3,0:T(8,128)} copy(f32[11,125,4,2,128]{4,1,0,3,2:T(8,128)} %bitcast) | data formatting | bytes 11264000 | tf_op jit(solution)/shard_map/all_to_all | solution.py:240
  84.2 6.2 %all_to_all.29 = f32[11,500,2,128]{3,1,2,0:T(8,128)} reshape(f32[11,4,125,2,128]{4,2,1,3,0:T(8,128)} %bitcast.25) | data formatting | bytes 11264000 | tf_op jit(solution)/shard_map/all_to_all | solution.py:240
  90.4 13.2 %convolution_bitcast_fusion = f32[500,500]{1,0:T(8,128)S(1)} fusion(f32[11,500,2,128]{3,1,2,0:T(8,128)} %all_to_all.29), kind=kOutput, calls=%fused_computation.2 | convolution fusion | flops 8448000000 | bytes 6632000 | tf_op jit(solution)/shard_map/dot_general | solution.py:241
  103.8 0.0 copy-start
  103.8 0.8 copy-done
  104.6 39.2 %shard_map.50 = f32[32,40,128]{2,1,0:T(8,128)} custom-call(f32[32,40,128]{2,1,0:T(8,128)} %bitcast.28), custom_call_target="tpu_custom_call" | custom-call | tf_op jit(solution)/shard_map/pallas_call | solution.py:131
  143.8 11.5 %shard_map.51 = (f32[64,512]{1,0:T(8,128)}, f32[500,64]{1,0:T(8,128)}) custom-call(f32[1280,128]{1,0:T(8,128)} %bitcast.27, f32[64,512]{1,0:T(8,128)} %pad.9.start_ref), custom_call_target="tpu_custom_call" | custom-call | tf_op jit(solution)/shard_map/pallas_call | solution.py:218
  155.3 0.0 copy-start.1
  155.3 4.6 %fusion.1 = f32[64,11,2,128]{3,0,2,1:T(8,128)S(1)} fusion(f32[11,500,2,128]{3,1,2,0:T(8,128)} %all_to_all.29, f32[64,512]{1,0:T(8,128)} %get-tuple-element.5), kind=kOutput, calls=%fused_computation.7 | convolution fusion | flops 540672000 | bytes 6483968 | tf_op jit(solution)/shard_map/dot_general | solution.py:256
  159.9 1.4 copy.18
  161.4 3.5 %all-to-all-start.1 = ((f32[64,11,2,128]{3,2,1,0:T(2,128)}), f32[64,11,2,128]{3,2,1,0:T(2,128)S(1)}, u32[]{:S(2)}, u32[]{:S(2)}) async-start(f32[64,11,2,128]{3,2,1,0:T(2,128)} %copy.18), calls=%async_computation.1 | async-start | bytes 1441792 | tf_op jit(solution)/shard_map/all_to_all | solution.py:259
  164.9 0.0 copy-done.1
  164.9 0.8 copy.20
  165.6 10.2 %all-to-all-done.1 = f32[64,11,2,128]{3,2,1,0:T(2,128)S(1)} async-done(((f32[64,11,2,128]{3,2,1,0:T(2,128)}), f32[64,11,2,128]{3,2,1,0:T(2,128)S(1)}, u32[]{:S(2)}, u32[]{:S(2)}) %all-to-all-start.1) | async-done | bytes 720928 | tf_op jit(solution)/shard_map/all_to_all | solution.py:259
  175.9 1.1 copy.19
  (9 shorter events, 0.1 us)
Async XLA Ops:
  7.3 5.3 %copy-start.2 = (f32[500,64]{0,1:T(8,128)S(1)}, f32[500,64]{0,1:T(8,128)}, u32[]{:S(2)}) copy-start(f32[500,64]{0,1:T(8,128)} %param.5) | copy-start | bytes 384004
  7.3 71.0 %all-to-all-start = ((f32[11,125,8,128]{3,1,0,2:T(8,128)}), f32[11,125,8,128]{3,1,0,2:T(8,128)}, u32[]{:S(2)}, u32[]{:S(2)}) async-start(f32[11,125,8,128]{3,1,0,2:T(8,128)} %copy.16), calls=%async_computation | async-start | bytes 11534336 | tf_op jit(solution)/shard_map/all_to_all | solution.py:240
  103.8 0.8 copy-start
  155.3 9.6 %copy-start.1 = (f32[500,64]{1,0:T(8,128)S(1)}, f32[500,64]{1,0:T(8,128)}, u32[]{:S(2)}) copy-start(f32[500,64]{1,0:T(8,128)} %get-tuple-element.12) | copy-start | bytes 384004
  161.4 14.5 %all-to-all-start.1 = ((f32[64,11,2,128]{3,2,1,0:T(2,128)}), f32[64,11,2,128]{3,2,1,0:T(2,128)S(1)}, u32[]{:S(2)}, u32[]{:S(2)}) async-start(f32[64,11,2,128]{3,2,1,0:T(2,128)} %copy.18), calls=%async_computation.1 | async-start | bytes 1441792 | tf_op jit(solution)/shard_map/all_to_all | solution.py:259

commit v2 on v1

v2 whole, which is shorter than its diff:
```python
import functools

import jax
import jax.numpy as jnp
from jax import lax
from jax.experimental import pallas as pl
from jax.experimental.pallas import tpu as pltpu
from jax.sharding import PartitionSpec as P

ITERS = 3
LANES = 128
SUB = 8
PANEL = 8
HIGHEST = lax.Precision.HIGHEST
MESH = pl.DeviceIdType.MESH


def flat_index(axes, sizes):
    flat = 0
    for name, size in zip(axes, sizes):
        flat = flat * size + lax.axis_index(name)
    return flat


def coords(flat, sizes):
    out = []
    for size in reversed(sizes):
        out.append(lax.rem(flat, size))
        flat = lax.div(flat, size)
    return tuple(reversed(out))


def greet(peers):
    barrier = pltpu.get_barrier_semaphore()
    for count, place in peers:
        for k in range(1, count):
            pl.semaphore_signal(barrier, inc=1, device_id=place(k), device_id_type=MESH)
    pl.semaphore_wait(barrier, sum(count - 1 for count, _ in peers))


def send(src, dst, sems, device):
    return pltpu.make_async_remote_copy(
        src_ref=src,
        dst_ref=dst,
        send_sem=sems[0],
        recv_sem=sems[1],
        device_id=device,
        device_id_type=MESH,
    )


def reduce_kernel(axes, sizes, g_ref, out_ref, recv_a, mine, recv_b, own, *sems):
    na, nb = g_ref.shape[0], g_ref.shape[1]
    rest = sizes[1:]
    a = lax.axis_index(axes[0])
    b = flat_index(axes[1:], rest)
    b_at = tuple(lax.axis_index(name) for name in axes[1:])

    def peer_a(k):
        return lax.rem(a + k, na)

    def peer_b(k):
        return lax.rem(b + k, nb)

    def dev_a(k):
        return (peer_a(k),) + b_at

    def dev_b(k):
        return (a,) + coords(peer_b(k), rest)

    greet([(na, dev_a), (nb, dev_b)])
    (s1, r1), (s2, r2), (s3, r3), (s4, r4) = [(sems[2 * i], sems[2 * i + 1]) for i in range(4)]

    first = [send(g_ref.at[peer_a(k)], recv_a.at[k], (s1.at[k], r1.at[k]), dev_a(k)) for k in range(1, na)]
    for copy in first:
        copy.start()
    for copy in first:
        copy.wait_recv()
    total = g_ref[pl.ds(a, 1)][0]
    for k in range(1, na):
        total = total + recv_a[k]
    mine[...] = total

    second = [send(mine.at[peer_b(k)], recv_b.at[k], (s2.at[k], r2.at[k]), dev_b(k)) for k in range(1, nb)]
    for copy in second:
        copy.start()
    for copy in second:
        copy.wait_recv()
    total = mine[pl.ds(b, 1)][0]
    for k in range(1, nb):
        total = total + recv_b[k]
    own[...] = total
    out_ref[pl.ds(a, 1), pl.ds(b, 1)] = total[None, None]

    third = [send(own, out_ref.at[a, b], (s3.at[k], r3.at[k]), dev_b(k)) for k in range(1, nb)]
    for copy in third:
        copy.start()
    for k in range(1, nb):
        came = lax.rem(b + nb - k, nb)
        send(own, out_ref.at[a, came], (s3.at[k], r3.at[k]), dev_b(k)).wait_recv()

    fourth = [send(out_ref.at[a], out_ref.at[a], (s4.at[k], r4.at[k]), dev_a(k)) for k in range(1, na)]
    for copy in fourth:
        copy.start()
    for k in range(1, na):
        came = lax.rem(a + na - k, na)
        send(out_ref.at[a], out_ref.at[came], (s4.at[k], r4.at[k]), dev_a(k)).wait_recv()
    for copy in first + second + third + fourth:
        copy.wait_send()


def all_reduce_rows(packed, axes, sizes):
    na = sizes[0]
    nb = 1
    for size in sizes[1:]:
        nb *= size
    rows = packed.shape[0] // (na * nb)
    block = (rows, LANES)
    dma = pltpu.SemaphoreType.DMA
    out = pl.pallas_call(
        functools.partial(reduce_kernel, axes, sizes),
        out_shape=jax.ShapeDtypeStruct((na, nb) + block, jnp.float32),
        in_specs=[pl.BlockSpec(memory_space=pltpu.VMEM)],
        out_specs=pl.BlockSpec(memory_space=pltpu.VMEM),
        scratch_shapes=[
            pltpu.VMEM((na, nb) + block, jnp.float32),
            pltpu.VMEM((nb,) + block, jnp.float32),
            pltpu.VMEM((nb,) + block, jnp.float32),
            pltpu.VMEM(block, jnp.float32),
            dma((na,)), dma((na,)), dma((nb,)), dma((nb,)),
            dma((nb,)), dma((nb,)), dma((na,)), dma((na,)),
        ],
        compiler_params=pltpu.CompilerParams(collective_id=0, has_side_effects=True),
    )(packed.reshape((na, nb) + block))
    return out.reshape(na * nb * rows, LANES)


def swap_kernel(axes, chunk, t_ref, buf, g_ref, acc, local_sem, send_sem, recv_sem):
    units, na, height = buf.shape[0], buf.shape[1], buf.shape[2]
    size = na * height
    m = size // LANES
    chunks = units // chunk
    a = lax.axis_index(axes[0])
    rest = tuple(lax.axis_index(name) for name in axes[1:])

    def peer(k):
        return lax.rem(a + k, na)

    def dev(k):
        return (peer(k),) + rest

    def go(c, k):
        return send(
            t_ref.at[pl.ds(peer(k) * units + c * chunk, chunk)],
            buf.at[pl.ds(c * chunk, chunk), a],
            (send_sem.at[c, k], recv_sem.at[c, k]),
            dev(k),
        )

    def come(c, k):
        return send(
            t_ref.at[pl.ds(c * chunk, chunk)],
            buf.at[pl.ds(c * chunk, chunk), lax.rem(a + na - k, na)],
            (send_sem.at[c, k], recv_sem.at[c, k]),
            dev(k),
        )

    def stay(c):
        return pltpu.make_async_copy(
            t_ref.at[pl.ds(a * units + c * chunk, chunk)],
            buf.at[pl.ds(c * chunk, chunk), a],
            local_sem.at[c],
        )

    greet([(na, dev)])

    def start(c, x):
        for k in range(1, na):
            go(c, k).start()
        stay(c).start()
        return x

    lax.fori_loop(0, chunks, start, 0)
    acc[...] = jnp.zeros_like(acc)

    def use(c, x):
        for k in range(1, na):
            come(c, k).wait_recv()
        stay(c).wait()
        x = jnp.concatenate(
            [buf[c * chunk + u].reshape(size, LANES) for u in range(chunk)], axis=1
        )
        for i in range(0, m, 2):
            top, low = i * LANES, min(i + 2, m) * LANES
            acc[top:low, top:] += lax.dot_general(
                x[top:low], x[top:], (((1,), (1,)), ((), ())),
                precision=HIGHEST, preferred_element_type=jnp.float32,
            )
        return 0

    lax.fori_loop(0, chunks, use, 0)
    t = 0
    for i in range(m):
        for j in range(i, m):
            g_ref[t * LANES:(t + 1) * LANES, :] = acc[
                i * LANES:(i + 1) * LANES, j * LANES:(j + 1) * LANES
            ]
            t += 1
    if t * LANES < g_ref.shape[0]:
        g_ref[t * LANES:, :] = jnp.zeros((g_ref.shape[0] - t * LANES, LANES), jnp.float32)

    def finish(c, x):
        for k in range(1, na):
            go(c, k).wait_send()
        return x

    lax.fori_loop(0, chunks, finish, 0)


def swap_and_gram(t, axes, sizes):
    na = sizes[0]
    n = 1
    for size in sizes:
        n *= size
    units, height = t.shape[0] // na, t.shape[1]
    m = na * height // LANES
    rows = -(-(m * (m + 1) // 2 * LANES) // (n * SUB)) * SUB
    chunk = 2 if units % 2 == 0 else 1
    vmem = pl.BlockSpec(memory_space=pltpu.VMEM)
    dma = pltpu.SemaphoreType.DMA
    return pl.pallas_call(
        functools.partial(swap_kernel, axes, chunk),
        out_shape=(
            jax.ShapeDtypeStruct((units, na, height, LANES), jnp.float32),
            jax.ShapeDtypeStruct((n * rows, LANES), jnp.float32),
        ),
        in_specs=[pl.BlockSpec(memory_space=pl.ANY)],
        out_specs=(vmem, vmem),
        scratch_shapes=[
            pltpu.VMEM((na * height, na * height), jnp.float32),
            dma((units // chunk,)),
            dma((units // chunk, na)),
            dma((units // chunk, na)),
        ],
        compiler_params=pltpu.CompilerParams(collective_id=1, has_side_effects=True),
    )(t)


def full(x):
    return jnp.broadcast_to(x, (SUB, LANES))


def inverse_lower(m, rank):
    groups = rank // SUB
    left = LANES - rank
    tiles = [m[g * SUB:(g + 1) * SUB, :] for g in range(groups)]
    sub = lax.broadcasted_iota(jnp.int32, (SUB, LANES), 0)
    done = []
    for g0 in range(groups):
        base = g0 * SUB
        cols = [
            [full(tiles[g][:, left + base + k:left + base + k + 1]) for g in range(g0, groups)]
            for k in range(SUB)
        ]
        rows = [full(tiles[g0][k:k + 1, :]) for k in range(SUB)]
        out = jnp.zeros((SUB, LANES), jnp.float32)
        for a in range(SUB):
            pivot = full(cols[a][0][a:a + 1, :])
            inv = 1.0 / pivot
            row = rows[a] * inv
            out = jnp.where(sub == a, rows[a] * lax.rsqrt(pivot), out)
            for b in range(a + 1, SUB):
                f = full(cols[a][0][b:b + 1, :])
                rows[b] = rows[b] - f * row
                fi = f * inv
                cols[b] = [cb - ca * fi for cb, ca in zip(cols[b], cols[a])]
            for i, g in enumerate(range(g0 + 1, groups)):
                tiles[g] = tiles[g] - cols[a][i + 1] * row
        done.append(out)
    return jnp.concatenate(done, axis=0)[:, :rank]


def iterate_kernel(m, rank, parts, p_ref, start_ref, bt_ref, f_ref, gram, wide):
    t = 0
    for i in range(m):
        for j in range(i, m):
            block = p_ref[t * LANES:(t + 1) * LANES, :]
            gram[i * LANES:(i + 1) * LANES, j * LANES:(j + 1) * LANES] = block
            if i != j:
                gram[j * LANES:(j + 1) * LANES, i * LANES:(i + 1) * LANES] = block.T
            t += 1
    wide[...] = jnp.zeros_like(wide)
    bt_ref[...] = start_ref[...]
    eye = (
        lax.broadcasted_iota(jnp.int32, (rank, LANES), 0)
        == lax.broadcasted_iota(jnp.int32, (rank, LANES), 1)
    ).astype(jnp.float32)

    def step(_, c):
        block = jnp.dot(bt_ref[...], gram[...], precision=HIGHEST, preferred_element_type=jnp.float32)
        wide[LANES - rank:, :] = block
        small = lax.dot_general(
            block, wide[...], (((1,), (1,)), ((), ())), precision=HIGHEST, preferred_element_type=jnp.float32
        )
        lower_inv = inverse_lower(small + eye, rank)
        bt_ref[...] = jnp.dot(lower_inv, block, precision=HIGHEST, preferred_element_type=jnp.float32)
        return c

    lax.fori_loop(0, ITERS, step, 0)
    basis = bt_ref[...].T
    height, cells = basis.shape[0] // parts, f_ref.shape[0] // parts
    for p in range(parts):
        f_ref[p * cells:(p + 1) * cells, :] = basis[p * height:p * height + cells, :]


def iterate(packed, start_basis, m, parts):
    cells, rank = start_basis.shape
    size = m * LANES
    start = start_basis.T.reshape(rank, parts, cells // parts)
    start = jnp.pad(start, ((0, 0), (0, 0), (0, (size - cells) // parts))).reshape(rank, size)
    vmem = pl.BlockSpec(memory_space=pltpu.VMEM)
    return pl.pallas_call(
        functools.partial(iterate_kernel, m, rank, parts),
        out_shape=(
            jax.ShapeDtypeStruct((rank, size), jnp.float32),
            jax.ShapeDtypeStruct((cells, rank), jnp.float32),
        ),
        in_specs=[vmem, vmem],
        out_specs=(vmem, vmem),
        scratch_shapes=[
            pltpu.VMEM((size, size), jnp.float32),
            pltpu.VMEM((LANES, size), jnp.float32),
        ],
    )(packed, start)


def solution(mesh):
    axes = tuple(mesh.axis_names)
    sizes = tuple(mesh.shape[a] for a in axes)

    def per_device(fields, var_scale, start_basis):
        na = sizes[0]
        nv, cells, nj, nk = fields.shape
        height = -(-cells // LANES) * LANES
        scaled = fields * var_scale[:, None, None, None]
        t = scaled.reshape(nv, cells, na, nj // na, nk).transpose(2, 0, 3, 1, 4)
        t = jnp.pad(t, ((0, 0), (0, 0), (0, 0), (0, height - cells), (0, 0)))
        swapped, packed = swap_and_gram(t.reshape(nv * nj, height, nk), axes, sizes)
        packed = all_reduce_rows(packed, axes, sizes)
        basis_t, factor = iterate(packed, start_basis, na * height // LANES, na)
        share = lax.dot_general(
            basis_t,
            swapped.reshape(-1, na * height, nk),
            (((1,), (1,)), ((), ())),
            precision=lax.Precision.HIGH,
        ).reshape(-1, nv, nj // na, nk)
        core = lax.all_to_all(share, "gx", split_axis=0, concat_axis=2, tiled=True)
        return factor, core

    in_specs = (P(None, "gx", "gy", "gz"), P(), P())
    out_specs = (P(), P("gx", None, "gy", "gz"))
    return jax.shard_map(
        per_device, mesh=mesh, in_specs=in_specs, out_specs=out_specs, check_vma=False
    )
```

time: 177 us -> 143 us (0.81)
  waiting for transfers between devices: 75.3 us -> 10.5 us
  Pallas kernels: 50.7 us -> 112 us
  matrix products: 17.9 us -> 4.68 us
  local copies, waits for them, and re-layouts: 20.6 us -> 8.17 us
  starting transfers between devices: 8.76 us -> 3.49 us
    all_to_all x1 -> x0, waiting for transfers between devices: 65.1 us -> none  [per_device(): lax.all_to_all(scaled, 'gx', split_axis=2, concat_axis=1, tiled=True)]
    pallas_call x2 -> x3, Pallas kernels: 50.7 us -> 112 us  [the longest x1 69.1 us: swap_and_gram(): pl.pallas_call(functools.partial(swap_kernel, axes, chunk), out_shape=(ja...]
    dot_general x2 -> x1, matrix products: 17.9 us -> 4.68 us  [per_device(): lax.dot_general(basis_t, swapped.reshape(-1, na * height, nk), (((1,), (1...]
    all_to_all x2 -> x0, local copies, waits for them, and re-layouts: 12.1 us -> none  [per_device(): lax.all_to_all(scaled, 'gx', split_axis=2, concat_axis=1, tiled=True)]
    all_to_all x1 -> x0, starting transfers between devices: 5.27 us -> none  [per_device(): lax.all_to_all(scaled, 'gx', split_axis=2, concat_axis=1, tiled=True)]
    mul x1 -> x0, local copies, waits for them, and re-layouts: 3.59 us -> none  [per_device(): scaled = fields * var_scale[:, None, None, None]]
    pad x1 -> x2, local copies, waits for them, and re-layouts: 0.67 us -> 2.96 us  [the longest x1 2.94 us: per_device(): t = jnp.pad(t, ((0, 0), (0, 0), (0, 0), (0, height - cells), (0, 0)))]
  transfers between devices with their start and end apart: 2 -> 1, of which waited for: 2 -> 1; matrix products, arithmetic and copies ran while one was open for 1% -> 1% of each run, Pallas kernels for 0% -> 0%
where the time goes in v2:
time: 143 us
  Pallas kernels  112 us (78%)
  waiting for transfers between devices  10.5 us (7%)
  local copies, waits for them, and re-layouts  8.17 us (6%)
  matrix products  4.68 us (3%)
  starting transfers between devices  3.49 us (2%)
  other arithmetic  3.03 us (2%)
    pallas_call x1, Pallas kernels, swap_and_gram(): pl.pallas_call(functools.partial(swap_kernel, axes, chunk), out_shape=(ja...  69.1 us
    pallas_call x1, Pallas kernels, all_reduce_rows(): pl.pallas_call(functools.partial(reduce_kernel, axes, sizes), out_shape=j...  31.6 us
    pallas_call x1, Pallas kernels, iterate(): pl.pallas_call(functools.partial(iterate_kernel, m, rank, parts), out_sha...  11.5 us
    all_to_all x1, waiting for transfers between devices, per_device(): core = lax.all_to_all(share, 'gx', split_axis=0, concat_axis=2, tiled=True)  10.5 us
    dot_general x1, matrix products, per_device(): lax.dot_general(basis_t, swapped.reshape(-1, na * height, nk), (((1,), (1...  4.68 us
    all_to_all x1, starting transfers between devices, per_device(): core = lax.all_to_all(share, 'gx', split_axis=0, concat_axis=2, tiled=True)  3.49 us
    mul x1, other arithmetic, per_device(): scaled = fields * var_scale[:, None, None, None]  3.03 us
    pad x1, local copies, waits for them, and re-layouts, per_device(): t = jnp.pad(t, ((0, 0), (0, 0), (0, 0), (0, height - cells), (0, 0)))  2.94 us
  transfers between devices with their start and end apart: 1, of which 1 were waited for; matrix products, arithmetic and copies ran while one was open for 1% of the time, Pallas kernels for 0%

profile of v2, /device:TPU:0, one launch (start us, length us, event | category | flops | bytes accessed | tf_op | source)
XLA Modules:
  0.0 142.8 jit_solution(1948860750779188187)
XLA Ops:
  0.6 3.0 %broadcast_multiply_fusion = f32[11,125,8,128]{3,2,1,0:T(8,128)S(1)} fusion(f32[11,125,8,128]{3,2,1,0:T(8,128)} %param.3, f32[11]{0:T(128)} %param.4), kind=kLoop, calls=%fused_computation.1 | loop fusion | flops 1408000 | bytes 11264044 | tf_op jit(solution)/shard_map/mul | solution.py:345
  3.7 1.1 copy.18
  4.8 2.9 %pad.8 = f32[4,11,2,128,128]{4,3,2,1,0:T(8,128)} pad(f32[4,11,2,125,128]{4,3,2,1,0:T(8,128)S(1)} %bitcast.29, f32[]{:T(128)} %constant.2.clone.1), padding=0_0x0_0x0_0x0_3x0_0 | pad | bytes 11399172 | tf_op jit(solution)/shard_map/jit(_pad)/pad | solution.py:347
  7.7 0.0 copy-start.1
  7.7 69.1 %shard_map.50 = (f32[22,4,128,128]{3,2,1,0:T(8,128)}, f32[1280,128]{1,0:T(8,128)}) custom-call(f32[88,128,128]{2,1,0:T(8,128)} %bitcast.28), custom_call_target="tpu_custom_call" | custom-call | tf_op jit(solution)/shard_map/pallas_call | solution.py:231
  76.8 31.6 %shard_map.51 = f32[4,8,40,128]{3,2,1,0:T(8,128)} custom-call(f32[4,8,40,128]{3,2,1,0:T(8,128)} %bitcast.35), custom_call_target="tpu_custom_call" | custom-call | tf_op jit(solution)/shard_map/pallas_call | solution.py:120
  108.4 0.0 copy-done.1
  108.4 0.1 reshape.32
  108.6 0.7 copy.19
  109.3 11.5 %shard_map.52 = (f32[64,512]{1,0:T(8,128)}, f32[500,64]{1,0:T(8,128)}) custom-call(f32[1280,128]{1,0:T(8,128)} %bitcast.33, f32[64,512]{1,0:T(8,128)} %bitcast.37), custom_call_target="tpu_custom_call" | custom-call | tf_op jit(solution)/shard_map/pallas_call | solution.py:322
  120.7 0.0 copy-start
  120.7 4.7 %fusion = f32[64,11,2,128]{3,0,2,1:T(8,128)S(1)} fusion(f32[11,2,128,512]{2,3,1,0:T(8,128)} %bitcast.31, f32[64,512]{1,0:T(8,128)} %get-tuple-element.8), kind=kOutput, calls=%fused_computation.3 | convolution fusion | flops 553648128 | bytes 6619136 | tf_op jit(solution)/shard_map/dot_general | solution.py:351
  125.4 1.4 copy.11
  126.8 3.5 %all-to-all-start = ((f32[64,11,2,128]{3,2,1,0:T(2,128)}), f32[64,11,2,128]{3,2,1,0:T(2,128)S(1)}, u32[]{:S(2)}, u32[]{:S(2)}) async-start(f32[64,11,2,128]{3,2,1,0:T(2,128)} %copy.11), calls=%async_computation | async-start | bytes 1441792 | tf_op jit(solution)/shard_map/all_to_all | solution.py:357
  130.3 0.0 copy-done
  130.3 0.8 copy.13
  131.1 10.5 %all-to-all-done = f32[64,11,2,128]{3,2,1,0:T(2,128)S(1)} async-done(((f32[64,11,2,128]{3,2,1,0:T(2,128)}), f32[64,11,2,128]{3,2,1,0:T(2,128)S(1)}, u32[]{:S(2)}, u32[]{:S(2)}) %all-to-all-start) | async-done | bytes 720928 | tf_op jit(solution)/shard_map/all_to_all | solution.py:357
  141.6 1.1 copy.12
  (1 shorter events, 0.0 us)
Async XLA Ops:
  7.7 100.7 %copy-start.1 = (f32[500,64]{0,1:T(8,128)S(1)}, f32[500,64]{0,1:T(8,128)}, u32[]{:S(2)}) copy-start(f32[500,64]{0,1:T(8,128)} %param.5) | copy-start | bytes 384004
  120.7 9.6 %copy-start = (f32[500,64]{1,0:T(8,128)S(1)}, f32[500,64]{1,0:T(8,128)}, u32[]{:S(2)}) copy-start(f32[500,64]{1,0:T(8,128)} %get-tuple-element.12) | copy-start | bytes 384004
  126.8 14.8 %all-to-all-start = ((f32[64,11,2,128]{3,2,1,0:T(2,128)}), f32[64,11,2,128]{3,2,1,0:T(2,128)S(1)}, u32[]{:S(2)}, u32[]{:S(2)}) async-start(f32[64,11,2,128]{3,2,1,0:T(2,128)} %copy.11), calls=%async_computation | async-start | bytes 1441792 | tf_op jit(solution)/shard_map/all_to_all | solution.py:357

commit v3 on v2

--- a/solution.py
+++ b/solution.py
@@ -135,7 +135,7 @@
     return out.reshape(na * nb * rows, LANES)
 
 
-def swap_kernel(axes, chunk, t_ref, buf, g_ref, acc, local_sem, send_sem, recv_sem):
+def swap_kernel(axes, chunk, cells, f_ref, scale_ref, buf, g_ref, acc, fbuf, t_ref, load_sem, local_sem, send_sem, recv_sem):
     units, na, height = buf.shape[0], buf.shape[1], buf.shape[2]
     size = na * height
     m = size // LANES
@@ -151,7 +151,7 @@
 
     def go(c, k):
         return send(
-            t_ref.at[pl.ds(peer(k) * units + c * chunk, chunk)],
+            t_ref.at[c, pl.ds(peer(k) * chunk, chunk)],
             buf.at[pl.ds(c * chunk, chunk), a],
             (send_sem.at[c, k], recv_sem.at[c, k]),
             dev(k),
@@ -159,7 +159,7 @@
 
     def come(c, k):
         return send(
-            t_ref.at[pl.ds(c * chunk, chunk)],
+            t_ref.at[c, pl.ds(a * chunk, chunk)],
             buf.at[pl.ds(c * chunk, chunk), lax.rem(a + na - k, na)],
             (send_sem.at[c, k], recv_sem.at[c, k]),
             dev(k),
@@ -167,20 +167,40 @@
 
     def stay(c):
         return pltpu.make_async_copy(
-            t_ref.at[pl.ds(a * units + c * chunk, chunk)],
+            t_ref.at[c, pl.ds(a * chunk, chunk)],
             buf.at[pl.ds(c * chunk, chunk), a],
             local_sem.at[c],
         )
 
+    nj = na * chunk
+
+    def load(c):
+        return pltpu.make_async_copy(f_ref.at[c], fbuf.at[c], load_sem.at[c])
+
+    def fetch(c, x):
+        load(c).start()
+        return x
+
+    lax.fori_loop(0, chunks, fetch, 0)
     greet([(na, dev)])
 
-    def start(c, x):
+    def start(c):
         for k in range(1, na):
             go(c, k).start()
         stay(c).start()
-        return x
-
-    lax.fori_loop(0, chunks, start, 0)
+
+    def turn(c, x):
+        load(c).wait()
+        scale = scale_ref[c]
+        for j in range(nj):
+            t_ref[c, j, :cells, :] = fbuf[c, pl.ds(j, cells, stride=nj), :] * scale
+            if cells < height:
+                t_ref[c, j, cells:, :] = jnp.zeros((height - cells, LANES), jnp.float32)
+        pl.when(c > 0)(lambda: start(c - 1))
+        return x
+
+    lax.fori_loop(0, chunks, turn, 0)
+    start(chunks - 1)
     acc[...] = jnp.zeros_like(acc)
 
     def use(c, x):
@@ -217,33 +237,37 @@
     lax.fori_loop(0, chunks, finish, 0)
 
 
-def swap_and_gram(t, axes, sizes):
+def swap_and_gram(fields, var_scale, height, axes, sizes):
     na = sizes[0]
     n = 1
     for size in sizes:
         n *= size
-    units, height = t.shape[0] // na, t.shape[1]
+    nv, cells, nj, nk = fields.shape
+    chunk = nj // na
+    units = nv * chunk
     m = na * height // LANES
     rows = -(-(m * (m + 1) // 2 * LANES) // (n * SUB)) * SUB
-    chunk = 2 if units % 2 == 0 else 1
     vmem = pl.BlockSpec(memory_space=pltpu.VMEM)
     dma = pltpu.SemaphoreType.DMA
     return pl.pallas_call(
-        functools.partial(swap_kernel, axes, chunk),
+        functools.partial(swap_kernel, axes, chunk, cells),
         out_shape=(
             jax.ShapeDtypeStruct((units, na, height, LANES), jnp.float32),
             jax.ShapeDtypeStruct((n * rows, LANES), jnp.float32),
         ),
-        in_specs=[pl.BlockSpec(memory_space=pl.ANY)],
+        in_specs=[pl.BlockSpec(memory_space=pl.ANY), pl.BlockSpec(memory_space=pltpu.SMEM)],
         out_specs=(vmem, vmem),
         scratch_shapes=[
             pltpu.VMEM((na * height, na * height), jnp.float32),
-            dma((units // chunk,)),
-            dma((units // chunk, na)),
-            dma((units // chunk, na)),
+            pltpu.VMEM((nv, cells * nj, LANES), jnp.float32),
+            pltpu.VMEM((nv, nj, height, LANES), jnp.float32),
+            dma((nv,)),
+            dma((nv,)),
+            dma((nv, na)),
+            dma((nv, na)),
         ],
         compiler_params=pltpu.CompilerParams(collective_id=1, has_side_effects=True),
-    )(t)
+    )(fields.reshape(nv, cells * nj, nk), var_scale)
 
 
 def full(x):
@@ -334,6 +358,111 @@
     )(packed, start)
 
 
+def core_kernel(axes, nv, bt_ref, x_ref, out_ref, xbuf, share, recv, local_sem, send_sem, recv_sem):
+    units, size = xbuf.shape[0], xbuf.shape[1]
+    na, steps, ranks = share.shape[0], recv_sem.shape[0], share.shape[2]
+    width = units // steps
+    nj2 = units // nv
+    a = lax.axis_index(axes[0])
+    rest = tuple(lax.axis_index(name) for name in axes[1:])
+
+    def peer(k):
+        return lax.rem(a + k, na)
+
+    def dev(k):
+        return (peer(k),) + rest
+
+    def load(c):
+        at = pl.ds(c * width, width)
+        return pltpu.make_async_copy(x_ref.at[at], xbuf.at[at], local_sem.at[c])
+
+    def go(c, k, came):
+        at = pl.ds(c * width, width)
+        sems = (send_sem.at[c, k], recv_sem.at[c, k])
+        return send(share.at[peer(k), at], recv.at[came, at], sems, dev(k))
+
+    def start(c, x):
+        load(c).start()
+        return x
+
+    lax.fori_loop(0, steps, start, 0)
+    greet([(na, dev)])
+    bt = bt_ref[...]
+    bt_hi = bt.astype(jnp.bfloat16)
+    bt_lo = (bt - bt_hi.astype(jnp.float32)).astype(jnp.bfloat16)
+    both = jnp.concatenate([bt_hi, bt_lo], axis=0)
+    rank = bt.shape[0]
+
+    def mul(c, x):
+        load(c).wait()
+        x = jnp.concatenate([xbuf[c * width + u] for u in range(width)], axis=1)
+        hi = x.astype(jnp.bfloat16)
+        lo = (x - hi.astype(jnp.float32)).astype(jnp.bfloat16)
+        y = jnp.dot(both, hi, preferred_element_type=jnp.float32)
+        y = y[:rank] + y[rank:] + jnp.dot(bt_hi, lo, preferred_element_type=jnp.float32)
+        for p in range(na):
+            for u in range(width):
+                share[p, c * width + u] = y[p * ranks:(p + 1) * ranks, u * LANES:(u + 1) * LANES]
+
+        @pl.when(c > 0)
+        def _():
+            for k in range(1, na):
+                go(c - 1, k, a).start()
+
+        return 0
+
+    lax.fori_loop(0, steps, mul, 0)
+    for k in range(1, na):
+        go(steps - 1, k, a).start()
+    stride = nv * na * nj2
+
+    def place(c, x):
+        for k in range(na):
+            came = lax.rem(a + na - k, na)
+            if k:
+                go(c, k, came).wait_recv()
+            for u in range(width):
+                unit = c * width + u
+                row = lax.div(unit, nj2) * (na * nj2) + came * nj2 + lax.rem(unit, nj2)
+                value = recv[came, unit] if k else share[a, unit]
+                out_ref[pl.ds(row, ranks, stride=stride), :] = value
+        return x
+
+    lax.fori_loop(0, steps, place, 0)
+
+    def finish(c, x):
+        for k in range(1, na):
+            go(c, k, a).wait_send()
+        return x
+
+    lax.fori_loop(0, steps, finish, 0)
+
+
+def core_of(basis_t, swapped, nv, axes, sizes):
+    na = sizes[0]
+    units, size, _ = swapped.shape
+    ranks = basis_t.shape[0] // na
+    width = 2 if units % 2 == 0 else 1
+    steps = units // width
+    vmem = pl.BlockSpec(memory_space=pltpu.VMEM)
+    dma = pltpu.SemaphoreType.DMA
+    return pl.pallas_call(
+        functools.partial(core_kernel, axes, nv),
+        out_shape=jax.ShapeDtypeStruct((ranks * units * na, LANES), jnp.float32),
+        in_specs=[vmem, pl.BlockSpec(memory_space=pl.ANY)],
+        out_specs=vmem,
+        scratch_shapes=[
+            pltpu.VMEM((units, size, LANES), jnp.float32),
+            pltpu.VMEM((na, units, ranks, LANES), jnp.float32),
+            pltpu.VMEM((na, units, ranks, LANES), jnp.float32),
+            dma((steps,)),
+            dma((steps, na)),
+            dma((steps, na)),
+        ],
+        compiler_params=pltpu.CompilerParams(collective_id=2, has_side_effects=True),
+    )(basis_t, swapped)
+
+
 def solution(mesh):
     axes = tuple(mesh.axis_names)
     sizes = tuple(mesh.shape[a] for a in axes)
@@ -342,19 +471,11 @@
         na = sizes[0]
         nv, cells, nj, nk = fields.shape
         height = -(-cells // LANES) * LANES
-        scaled = fields * var_scale[:, None, None, None]
-        t = scaled.reshape(nv, cells, na, nj // na, nk).transpose(2, 0, 3, 1, 4)
-        t = jnp.pad(t, ((0, 0), (0, 0), (0, 0), (0, height - cells), (0, 0)))
-        swapped, packed = swap_and_gram(t.reshape(nv * nj, height, nk), axes, sizes)
+        swapped, packed = swap_and_gram(fields, var_scale, height, axes, sizes)
         packed = all_reduce_rows(packed, axes, sizes)
         basis_t, factor = iterate(packed, start_basis, na * height // LANES, na)
-        share = lax.dot_general(
-            basis_t,
-            swapped.reshape(-1, na * height, nk),
-            (((1,), (1,)), ((), ())),
-            precision=lax.Precision.HIGH,
-        ).reshape(-1, nv, nj // na, nk)
-        core = lax.all_to_all(share, "gx", split_axis=0, concat_axis=2, tiled=True)
+        core = core_of(basis_t, swapped.reshape(-1, na * height, nk), nv, axes, sizes)
+        core = core.reshape(-1, nv, nj, nk)
         return factor, core
 
     in_specs = (P(None, "gx", "gy", "gz"), P(), P())

time: 143 us -> 133 us (0.930)
  Pallas kernels: 112 us -> 128 us
  waiting for transfers between devices: 10.5 us -> 0 us
  matrix products: 4.68 us -> 0 us
  local copies, waits for them, and re-layouts: 8.17 us -> 3.62 us
  starting transfers between devices: 3.49 us -> 0 us
  other arithmetic: 3.03 us -> 0 us
    pallas_call x1 -> x2, Pallas kernels: 69.1 us -> 85.4 us  [the longest x1 70.3 us: swap_and_gram(): pl.pallas_call(functools.partial(swap_kernel, axes, chunk, cells), out_sh...]
    all_to_all x1 -> x0, waiting for transfers between devices: 10.5 us -> none  [per_device(): core = lax.all_to_all(share, 'gx', split_axis=0, concat_axis=2, tiled=True)]
    dot_general x1 -> x0, matrix products: 4.68 us -> none  [per_device(): lax.dot_general(basis_t, swapped.reshape(-1, na * height, nk), (((1,), (1...]
    all_to_all x1 -> x0, starting transfers between devices: 3.49 us -> none  [per_device(): core = lax.all_to_all(share, 'gx', split_axis=0, concat_axis=2, tiled=True)]
    mul x1 -> x0, other arithmetic: 3.03 us -> none  [per_device(): scaled = fields * var_scale[:, None, None, None]]
    pad x1 -> x0, local copies, waits for them, and re-layouts: 2.94 us -> none  [per_device(): t = jnp.pad(t, ((0, 0), (0, 0), (0, 0), (0, height - cells), (0, 0)))]
    unnamed x6 -> x7, local copies, waits for them, and re-layouts: 1.45 us -> 3.46 us
  transfers between devices with their start and end apart: 1 -> 0, of which waited for: 1 -> 0; matrix products, arithmetic and copies ran while one was open for 1% -> 0% of each run, Pallas kernels for 0% -> 0%
where the time goes in v3:
time: 133 us
  Pallas kernels  128 us (96%)
  local copies, waits for them, and re-layouts  3.62 us (3%)
    pallas_call x1, Pallas kernels, swap_and_gram(): pl.pallas_call(functools.partial(swap_kernel, axes, chunk, cells), out_sh...  70.3 us
    pallas_call x1, Pallas kernels, all_reduce_rows(): pl.pallas_call(functools.partial(reduce_kernel, axes, sizes), out_shape=j...  31.5 us
    pallas_call x1, Pallas kernels, core_of(): pl.pallas_call(functools.partial(core_kernel, axes, nv), out_shape=jax.Sh...  15.1 us
    pallas_call x1, Pallas kernels, iterate(): pl.pallas_call(functools.partial(iterate_kernel, m, rank, parts), out_sha...  11.4 us
    unnamed x7, local copies, waits for them, and re-layouts  3.46 us

profile of v3, /device:TPU:0, one launch (start us, length us, event | category | flops | bytes accessed | tf_op | source)
XLA Modules:
  0.0 132.6 jit_solution(8763196001473565938)
XLA Ops:
  0.6 0.0 copy-start.1
  0.6 70.3 %shard_map.50 = (f32[22,4,128,128]{3,2,1,0:T(8,128)}, f32[1280,128]{1,0:T(8,128)}) custom-call(f32[11,1000,128]{2,1,0:T(8,128)} %bitcast.11, f32[11]{0:T(128)} %scale_ref.1), custom_call_target="tpu_custom_call" | custom-call | tf_op jit(solution)/shard_map/pallas_call | solution.py:252
  70.9 31.5 %shard_map.51 = f32[4,8,40,128]{3,2,1,0:T(8,128)} custom-call(f32[4,8,40,128]{3,2,1,0:T(8,128)} %bitcast.14), custom_call_target="tpu_custom_call" | custom-call | tf_op jit(solution)/shard_map/pallas_call | solution.py:120
  102.4 0.0 copy-done.1
  102.4 0.1 reshape.28
  102.6 0.7 copy.8
  103.3 11.4 %shard_map.52 = (f32[64,512]{1,0:T(8,128)}, f32[500,64]{1,0:T(8,128)}) custom-call(f32[1280,128]{1,0:T(8,128)} %bitcast.13, f32[64,512]{1,0:T(8,128)} %bitcast.16), custom_call_target="tpu_custom_call" | custom-call | tf_op jit(solution)/shard_map/pallas_call | solution.py:346
  114.7 0.0 copy-start
  114.7 15.1 %shard_map.53 = f32[1408,128]{1,0:T(8,128)} custom-call(f32[64,512]{1,0:T(8,128)} %get-tuple-element.8.bt_ref, f32[22,512,128]{2,1,0:T(8,128)} %bitcast.10), custom_call_target="tpu_custom_call" | custom-call | tf_op jit(solution)/shard_map/pallas_call | solution.py:449
  129.8 0.0 copy-done
  129.8 0.8 copy.5
  130.6 2.0 %copy.10 = f32[16,11,8,128]{3,2,1,0:T(8,128)} copy(f32[16,11,8,128]{3,2,1,0:T(8,128)} %bitcast.12) | data formatting | bytes 1441792
  (1 shorter events, 0.0 us)
Async XLA Ops:
  0.6 101.8 %copy-start.1 = (f32[500,64]{0,1:T(8,128)S(1)}, f32[500,64]{0,1:T(8,128)}, u32[]{:S(2)}) copy-start(f32[500,64]{0,1:T(8,128)} %param.5) | copy-start | bytes 384004
  114.7 15.1 %copy-start = (f32[500,64]{1,0:T(8,128)S(1)}, f32[500,64]{1,0:T(8,128)}, u32[]{:S(2)}) copy-start(f32[500,64]{1,0:T(8,128)} %get-tuple-element.10) | copy-start | bytes 384004

commit v4 on v3

--- a/solution.py
+++ b/solution.py
@@ -71,41 +71,50 @@
     greet([(na, dev_a), (nb, dev_b)])
     (s1, r1), (s2, r2), (s3, r3), (s4, r4) = [(sems[2 * i], sems[2 * i + 1]) for i in range(4)]
 
-    first = [send(g_ref.at[peer_a(k)], recv_a.at[k], (s1.at[k], r1.at[k]), dev_a(k)) for k in range(1, na)]
-    for copy in first:
+    order = list(range(1, nb)) + [0]
+    first = {
+        (k, q): send(g_ref.at[peer_a(k), peer_b(q)], recv_a.at[k, q], (s1.at[k, q], r1.at[k, q]), dev_a(k))
+        for q in order
+        for k in range(1, na)
+    }
+    for copy in first.values():
         copy.start()
-    for copy in first:
-        copy.wait_recv()
-    total = g_ref[pl.ds(a, 1)][0]
-    for k in range(1, na):
-        total = total + recv_a[k]
-    mine[...] = total
-
-    second = [send(mine.at[peer_b(k)], recv_b.at[k], (s2.at[k], r2.at[k]), dev_b(k)) for k in range(1, nb)]
-    for copy in second:
-        copy.start()
-    for copy in second:
-        copy.wait_recv()
-    total = mine[pl.ds(b, 1)][0]
-    for k in range(1, nb):
-        total = total + recv_b[k]
+    second = {
+        q: send(mine.at[q], recv_b.at[q], (s2.at[q], r2.at[q]), dev_b(q)) for q in range(1, nb)
+    }
+    for q in order:
+        for k in range(1, na):
+            first[k, q].wait_recv()
+        total = g_ref[a, peer_b(q)]
+        for k in range(1, na):
+            total = total + recv_a[k, q]
+        mine[q] = total
+        if q:
+            second[q].start()
+    for q in range(1, nb):
+        second[q].wait_recv()
+        total = total + recv_b[q]
     own[...] = total
-    out_ref[pl.ds(a, 1), pl.ds(b, 1)] = total[None, None]
-
-    third = [send(own, out_ref.at[a, b], (s3.at[k], r3.at[k]), dev_b(k)) for k in range(1, nb)]
+    out_ref[a, b] = total
+
+    third = [send(own, out_ref.at[a, b], (s3.at[q], r3.at[q]), dev_b(q)) for q in range(1, nb)]
     for copy in third:
         copy.start()
-    for k in range(1, nb):
-        came = lax.rem(b + nb - k, nb)
-        send(own, out_ref.at[a, came], (s3.at[k], r3.at[k]), dev_b(k)).wait_recv()
-
-    fourth = [send(out_ref.at[a], out_ref.at[a], (s4.at[k], r4.at[k]), dev_a(k)) for k in range(1, na)]
-    for copy in fourth:
-        copy.start()
-    for k in range(1, na):
-        came = lax.rem(a + na - k, na)
-        send(out_ref.at[a], out_ref.at[came], (s4.at[k], r4.at[k]), dev_a(k)).wait_recv()
-    for copy in first + second + third + fourth:
+    fourth = []
+    for q in range(nb):
+        came = lax.rem(b + nb - q, nb)
+        if q:
+            send(own, out_ref.at[a, came], (s3.at[q], r3.at[q]), dev_b(q)).wait_recv()
+        for k in range(1, na):
+            block = own if q == 0 else out_ref.at[a, came]
+            fourth.append(send(block, out_ref.at[a, came], (s4.at[k, q], r4.at[k, q]), dev_a(k)))
+            fourth[-1].start()
+    for q in range(nb):
+        came = lax.rem(b + nb - q, nb)
+        for k in range(1, na):
+            came_a = lax.rem(a + na - k, na)
+            send(own, out_ref.at[came_a, came], (s4.at[k, q], r4.at[k, q]), dev_a(k)).wait_recv()
+    for copy in list(first.values()) + list(second.values()) + third + fourth:
         copy.wait_send()
 
 
@@ -127,8 +136,8 @@
             pltpu.VMEM((nb,) + block, jnp.float32),
             pltpu.VMEM((nb,) + block, jnp.float32),
             pltpu.VMEM(block, jnp.float32),
-            dma((na,)), dma((na,)), dma((nb,)), dma((nb,)),
-            dma((nb,)), dma((nb,)), dma((na,)), dma((na,)),
+            dma((na, nb)), dma((na, nb)), dma((nb,)), dma((nb,)),
+            dma((nb,)), dma((nb,)), dma((na, nb)), dma((na, nb)),
         ],
         compiler_params=pltpu.CompilerParams(collective_id=0, has_side_effects=True),
     )(packed.reshape((na, nb) + block))
@@ -331,10 +340,10 @@
         return c
 
     lax.fori_loop(0, ITERS, step, 0)
-    basis = bt_ref[...].T
-    height, cells = basis.shape[0] // parts, f_ref.shape[0] // parts
-    for p in range(parts):
-        f_ref[p * cells:(p + 1) * cells, :] = basis[p * height:p * height + cells, :]
+    height, cells = bt_ref.shape[1] // parts, f_ref.shape[1] // parts
+    f_ref[...] = jnp.concatenate(
+        [bt_ref[:, p * height:p * height + cells] for p in range(parts)], axis=1
+    )
 
 
 def iterate(packed, start_basis, m, parts):
@@ -347,7 +356,7 @@
         functools.partial(iterate_kernel, m, rank, parts),
         out_shape=(
             jax.ShapeDtypeStruct((rank, size), jnp.float32),
-            jax.ShapeDtypeStruct((cells, rank), jnp.float32),
+            jax.ShapeDtypeStruct((rank, cells), jnp.float32),
         ),
         in_specs=[vmem, vmem],
         out_specs=(vmem, vmem),
@@ -476,7 +485,7 @@
         basis_t, factor = iterate(packed, start_basis, na * height // LANES, na)
         core = core_of(basis_t, swapped.reshape(-1, na * height, nk), nv, axes, sizes)
         core = core.reshape(-1, nv, nj, nk)
-        return factor, core
+        return factor.T, core
 
     in_specs = (P(None, "gx", "gy", "gz"), P(), P())
     out_specs = (P(), P("gx", None, "gy", "gz"))

time: 133 us -> 131 us (0.985)
    unnamed x7 -> x4, local copies, waits for them, and re-layouts: 3.46 us -> 2.68 us
where the time goes in v4:
time: 131 us
  Pallas kernels  127 us (97%)
  local copies, waits for them, and re-layouts  2.84 us (2%)
    pallas_call x1, Pallas kernels, swap_and_gram(): pl.pallas_call(functools.partial(swap_kernel, axes, chunk, cells), out_sh...  70.3 us
    pallas_call x1, Pallas kernels, all_reduce_rows(): pl.pallas_call(functools.partial(reduce_kernel, axes, sizes), out_shape=j...  31.6 us
    pallas_call x1, Pallas kernels, core_of(): pl.pallas_call(functools.partial(core_kernel, axes, nv), out_shape=jax.Sh...  14 us
    pallas_call x1, Pallas kernels, iterate(): pl.pallas_call(functools.partial(iterate_kernel, m, rank, parts), out_sha...  11.4 us
    unnamed x4, local copies, waits for them, and re-layouts  2.68 us

profile of v4, /device:TPU:0, one launch (start us, length us, event | category | flops | bytes accessed | tf_op | source)
XLA Modules:
  0.0 130.8 jit_solution(15867506194875194669)
XLA Ops:
  0.6 0.0 copy-start
  0.6 70.3 %shard_map.50 = (f32[22,4,128,128]{3,2,1,0:T(8,128)}, f32[1280,128]{1,0:T(8,128)}) custom-call(f32[11,1000,128]{2,1,0:T(8,128)} %bitcast.12, f32[11]{0:T(128)} %scale_ref.1), custom_call_target="tpu_custom_call" | custom-call | tf_op jit(solution)/shard_map/pallas_call | solution.py:261
  70.9 31.6 %shard_map.51 = f32[4,8,40,128]{3,2,1,0:T(8,128)} custom-call(f32[4,8,40,128]{3,2,1,0:T(8,128)} %bitcast.15), custom_call_target="tpu_custom_call" | custom-call | tf_op jit(solution)/shard_map/pallas_call | solution.py:129
  102.5 0.0 copy-done
  102.5 0.1 reshape.28
  102.7 0.7 copy.7
  103.4 11.4 %shard_map.52 = (f32[64,512]{1,0:T(8,128)}, f32[64,500]{1,0:T(8,128)}) custom-call(f32[1280,128]{1,0:T(8,128)} %bitcast.14, f32[64,512]{1,0:T(8,128)} %bitcast.17), custom_call_target="tpu_custom_call" | custom-call | tf_op jit(solution)/shard_map/pallas_call | solution.py:355
  114.8 14.0 %shard_map.53 = f32[1408,128]{1,0:T(8,128)} custom-call(f32[64,512]{1,0:T(8,128)} %get-tuple-element.8.bt_ref, f32[22,512,128]{2,1,0:T(8,128)} %bitcast.11), custom_call_target="tpu_custom_call" | custom-call | tf_op jit(solution)/shard_map/pallas_call | solution.py:458
  128.8 2.0 %copy.9 = f32[16,11,8,128]{3,2,1,0:T(8,128)} copy(f32[16,11,8,128]{3,2,1,0:T(8,128)} %bitcast.13) | data formatting | bytes 1441792
  (1 shorter events, 0.0 us)
Async XLA Ops:
  0.6 101.9 %copy-start = (f32[500,64]{0,1:T(8,128)S(1)}, f32[500,64]{0,1:T(8,128)}, u32[]{:S(2)}) copy-start(f32[500,64]{0,1:T(8,128)} %param.5) | copy-start | bytes 384004
